TPU v7x, 32 devices: a whole 2x2x4 slice. The times are simulated.
32 devices in a mesh: prow: 8 (over z, y), pcol: 4 (over x, core).
Axes of the slice: x: 2, y: 2, z: 4, core: 2. Of those that a mesh axis runs over, the one named last changes fastest.
Arguments:
- iface_tiles: int32 [32, 16], replicated, may hold values from 0 to 63, as said below
- interior_sizes: int32 [32], P(('prow', 'pcol')), may hold values from 128 to 512
- coupling: float32 [32, 512, 2048], P(('prow', 'pcol')), may hold values from -0.25 to 0.25
- factor_inverse: float32 [32, 512, 512], P(('prow', 'pcol')), as said below
- interface_block: float32 [8, 8, 4, 16, 128, 128], P('prow', None, 'pcol'), as said below
Outputs:
- schur: float32 [8, 8, 4, 16, 128, 128], P('prow', None, 'pcol')
- panel: float32 [8, 8, 128, 128], P('prow', None, 'pcol')
Inputs may be any that keep to these rules, and one draw needn't show every extreme that they name: `iface_tiles`: each row holds 16 distinct tile numbers; for every r, exactly 2 of them are r modulo 8; every tile number stands in exactly 8 rows. `factor_inverse`: each matrix is lower triangular with a diagonal between 0.25 and 1. `interface_block`: diagonal entries lie between 80 and 160; other entries are of order one.
All inputs are finite; a program needn't handle non-finite values.
Results may differ from a plain program's by a relative error of at most 0.0001.
Values sent between devices are 32-bit elements; how exact they have to be, the bound alone decides.
A program may use at most 128 MiB of HBM per device.

v0:
```python
import jax
import jax.numpy as jnp
from jax import lax
from jax.sharding import PartitionSpec as P


def broadcast(block, axis, owner):
    block = jnp.where(lax.axis_index(axis) == owner, block, jnp.zeros_like(block))
    return lax.psum(block, axis)


def solve_panel(diag_block, column):
    lower = jnp.linalg.cholesky(0.5 * (diag_block + diag_block.T))
    flat = column.reshape(-1, diag_block.shape[0])
    solved = jax.scipy.linalg.solve_triangular(lower, flat.T, lower=True)
    return solved.T.reshape(column.shape)


def shards(iface_tiles, interior_sizes, coupling, factor_inverse, interface_block):
    rows_grid = lax.axis_size("prow")
    cols_grid = lax.axis_size("pcol")
    prow_index = lax.axis_index("prow")
    pcol_index = lax.axis_index("pcol")
    self_index = prow_index * cols_grid + pcol_index
    domains = iface_tiles.shape[0]
    tile_count = iface_tiles.shape[1]
    tile_width = interface_block.shape[-1]
    local_rows = interface_block.shape[1]
    local_cols = interface_block.shape[3]
    rows_per = tile_count // rows_grid
    cols_per = tile_count // cols_grid
    share_rows = tile_width // cols_grid
    live_count = interior_sizes[0]
    own_coupling = coupling[0]
    own_factor = factor_inverse[0]
    interior = own_coupling.shape[0]
    interior_live = (lax.iota(jnp.int32, interior) < live_count)[:, None]
    masked = jnp.where(interior_live, own_coupling, 0.0)
    own_tiles = lax.dynamic_index_in_dim(iface_tiles, self_index, 0, keepdims=False)
    row_order = jnp.argsort(own_tiles % rows_grid, stable=True)
    col_order = jnp.argsort(own_tiles % cols_grid, stable=True)
    weighted = jnp.dot(
        own_factor, masked, precision=lax.Precision.HIGHEST, preferred_element_type=jnp.float32
    )
    weighted = jnp.where(interior_live, weighted, 0.0).reshape(interior, tile_count, tile_width)
    row_part = jnp.take(weighted, row_order, axis=1).reshape(
        interior, rows_grid, rows_per, tile_width
    )
    col_part = jnp.take(weighted, col_order, axis=1).reshape(
        interior, cols_grid, cols_per, tile_width
    )
    contribution = -jnp.einsum(
        "kprt,kqcu->pqrctu", row_part, col_part, precision=lax.Precision.HIGHEST
    )
    received = lax.all_to_all(
        contribution.reshape(rows_grid * cols_grid, rows_per, cols_per, tile_width, tile_width),
        ("prow", "pcol"),
        split_axis=0,
        concat_axis=0,
        tiled=True,
    )
    sorted_rows = jnp.take_along_axis(
        iface_tiles, jnp.argsort(iface_tiles % rows_grid, axis=1, stable=True), axis=1
    )
    sorted_rows = sorted_rows.reshape(domains, rows_grid, rows_per)
    sorted_cols = jnp.take_along_axis(
        iface_tiles, jnp.argsort(iface_tiles % cols_grid, axis=1, stable=True), axis=1
    )
    sorted_cols = sorted_cols.reshape(domains, cols_grid, cols_per)
    target_rows = lax.dynamic_index_in_dim(sorted_rows, prow_index, 1, keepdims=False) // rows_grid
    target_cols = lax.dynamic_index_in_dim(sorted_cols, pcol_index, 1, keepdims=False) // cols_grid
    slot_ids = (target_rows[:, :, None] * local_cols + target_cols[:, None, :]).reshape(-1)
    base_tiles = interface_block.reshape(local_rows * local_cols, tile_width, tile_width)
    summed = base_tiles.at[slot_ids].add(received.reshape(-1, tile_width, tile_width))
    schur = summed.reshape(interface_block.shape)
    column = summed.reshape(local_rows, local_cols, tile_width, tile_width)[:, 0]
    diag_block = broadcast(column[0], "prow", 0)
    factored = solve_panel(diag_block, column)
    panel = broadcast(factored, "pcol", 0)
    own_share = lax.dynamic_slice_in_dim(panel, pcol_index * share_rows, share_rows, 1)
    return (schur, own_share[None])


def solution(mesh):
    in_specs = (
        P(),
        P(("prow", "pcol")),
        P(("prow", "pcol"), None, None),
        P(("prow", "pcol"), None, None),
        P("prow", None, "pcol", None, None, None),
    )
    out_specs = (P("prow", None, "pcol", None, None, None), P("prow", None, "pcol", None))
    return jax.shard_map(shards, mesh=mesh, in_specs=in_specs, out_specs=out_specs, check_vma=False)
```

profile of v0, /device:TPU:0, one launch (start us, length us, event | category | flops | bytes accessed | tf_op | source)
XLA Modules:
  0.0 673.2 jit_solution(10466884502546801936)
XLA Ops:
  7.2 8.0 %copy.40 = f32[1,8,1,16,128,128]{5,4,3,2,1,0:T(8,128)} copy(f32[1,8,1,16,128,128]{5,4,3,2,1,0:T(8,128)} %param.13) | data formatting | bytes 16777216
  15.2 0.2 dynamic-slice_reduce_fusion
  15.4 1.2 sort.64
  16.6 1.2 sort.65
  18.6 16.4 %fusion.3 = f32[2048,512]{1,0:T(8,128)} fusion(f32[1,512,2048]{2,1,0:T(8,128)} %param.11, pred[512]{0:T(512)(128)(4,1)S(1)} %iota_compare_fusion.2, f32[1,512,512]{2,1,0:T(8,128)S(1)} %copy-done), kind=kOutput, calls=%fused_computation.9 | convolution fusion | flops 6444548096 | bytes 9437696 | tf_op jit(solution)/shard_map/dot_general | solution.py:42
  35.0 5.0 gather_fusion.2
  40.0 5.0 gather_fusion.3
  44.9 2.9 broadcast_select_fusion.1
  47.9 0.5 copy-done.3
  48.4 0.6 broadcast_select_fusion
  49.0 30.0 %negate_bitcast_fusion = f32[8,4,2,4,128,128]{4,5,2,0,3,1:T(8,128)} fusion(f32[512,4,4,128,1,1]{0,3,5,4,2,1:T(8,128)S(1)} %bitcast.89, f32[512,8,2,128,1,1]{0,3,2,1,5,4:T(8,128)S(1)} %bitcast.90), kind=kOutput, calls=%fused_computation.5 | convolution fusion | flops 25773998080 | bytes 25165824 | tf_op jit(solution)/shard_map/kprt,kqcu->pqrctu/dot_general | solution.py:52
  79.0 17.4 %copy.23 = f32[8,4,2,4,128,128]{5,4,3,2,1,0:T(8,128)} copy(f32[8,4,2,4,128,128]{4,5,2,0,3,1:T(8,128)} %negate_bitcast_fusion) | data formatting | bytes 33554432 | tf_op jit(solution)/shard_map/neg | solution.py:52
  96.4 7.5 %all-to-all-start = ((f32[32,2,4,128,128]{4,3,2,1,0:T(8,128)}), f32[32,2,4,128,128]{4,3,2,1,0:T(8,128)}, u32[]{:S(2)}, u32[]{:S(2)}) async-start(f32[32,2,4,128,128]{4,3,2,1,0:T(8,128)} %bitcast.86), calls=%async_computation | async-start | bytes 33554432 | tf_op jit(solution)/shard_map/all_to_all | solution.py:55
  103.9 0.0 all-reduce.3.cloned.1.call-start
  103.9 0.7 sort.63
  104.6 0.1 copy.19
  104.7 0.1 reshape.202
  104.8 3.9 gather_fusion.1
  108.7 0.1 reshape.205
  108.8 0.1 copy.20
  108.9 0.1 copy.21
  109.0 0.7 sort.62
  109.7 0.1 copy.16
  109.8 0.1 reshape.197
  109.9 3.9 gather_fusion
  113.8 0.1 reshape.200
  113.8 0.1 copy.17
  113.9 0.1 copy.18
  114.0 0.1 broadcast_add_fusion
  114.1 0.1 add.122
  114.3 362.2 %all-to-all-done = f32[32,2,4,128,128]{4,3,2,1,0:T(8,128)} async-done(((f32[32,2,4,128,128]{4,3,2,1,0:T(8,128)}), f32[32,2,4,128,128]{4,3,2,1,0:T(8,128)}, u32[]{:S(2)}, u32[]{:S(2)}) %all-to-all-start) | async-done | bytes 16777248 | tf_op jit(solution)/shard_map/all_to_all | solution.py:55
  476.4 51.2 %scatter_fusion = f32[128,128,128]{2,1,0:T(8,128)} fusion(f32[128,128,128]{2,1,0:T(8,128)} %bitcast.84, s32[256]{0:T(256)S(1)} %bitcast.95, f32[256,128,128]{2,1,0:T(8,128)} %bitcast.24), kind=kCustom, calls=%fused_computation.4 | custom fusion | flops 4194304 | bytes 50332672 | tf_op jit(solution)/shard_map/scatter-add | solution.py:74
  527.7 9.1 %copy.24 = f32[128,128,128]{1,2,0:T(8,128)} copy(f32[128,128,128]{2,1,0:T(8,128)} %scatter_fusion) | data formatting | bytes 16777216 | tf_op jit(solution)/shard_map/scatter-add | solution.py:74
  536.7 1.5 fusion.10
  538.2 0.0 all-reduce.3.cloned.1.call-update
  538.2 0.3 all-reduce.5.cloned.1.call-start
  538.5 65.0 %all-reduce.3.cloned.1.call-done = f32[128,128]{0,1:T(8,128)} async-done(((f32[128,128]{0,1:T(8,128)}), f32[128,128]{0,1:T(8,128)}) %all-reduce.3.cloned.1.call-update) | async-done | bytes 65552 | tf_op jit(solution)/shard_map/psum | solution.py:9
  603.5 0.9 copy.25
  604.5 0.9 fusion.13
  605.3 0.1 copy.26
  605.4 11.7 %cholesky.15 = f32[128,128]{1,0:T(8,128)S(1)} custom-call(f32[128,128]{1,0:T(8,128)S(1)} %fusion.12), custom_call_target="Cholesky" | custom-call | tf_op jit(solution)/shard_map/jit(cholesky)/cholesky | solution.py:13
  617.2 0.6 compare_reduce_fusion
  617.8 0.7 fusion.9
  618.5 9.8 %custom-call.7 = f32[1,128,128]{1,2,0:T(8,128)S(1)} custom-call(f32[1,128,128]{2,1,0:T(8,128)S(1)} %fusion.9), custom_call_target="InvertDiagBlocksLowerTriangular" | custom-call | tf_op jit(solution)/shard_map/jit(_solve_triangular)/triangular_solve | solution.py:15
  628.3 2.9 convolution_select_fusion
  631.2 0.0 all-reduce.5.cloned.1.call-update
  631.2 33.5 %all-reduce.5.cloned.1.call-done = f32[8,128,128]{2,1,0:T(8,128)} async-done(((f32[8,128,128]{2,1,0:T(8,128)}), f32[8,128,128]{2,1,0:T(8,128)}) %all-reduce.5.cloned.1.call-update) | async-done | bytes 524304 | tf_op jit(solution)/shard_map/psum | solution.py:9
  664.7 1.6 dynamic-slice_bitcast_fusion
  (27 shorter events, 0.2 us)
Async XLA Ops:
  7.2 11.4 %copy-start = (f32[1,512,512]{2,1,0:T(8,128)S(1)}, f32[1,512,512]{2,1,0:T(8,128)}, u32[]{:S(2)}) copy-start(f32[1,512,512]{2,1,0:T(8,128)} %param.12) | copy-start | bytes 3145732
  7.2 8.0 %copy-start.2 = (s32[32,16]{0,1:T(8,128)S(1)}, s32[32,16]{0,1:T(8,128)}, u32[]{:S(2)}) copy-start(s32[32,16]{0,1:T(8,128)} %param.9) | copy-start | bytes 6148
  44.9 3.4 copy-start.3
  96.4 380.1 %all-to-all-start = ((f32[32,2,4,128,128]{4,3,2,1,0:T(8,128)}), f32[32,2,4,128,128]{4,3,2,1,0:T(8,128)}, u32[]{:S(2)}, u32[]{:S(2)}) async-start(f32[32,2,4,128,128]{4,3,2,1,0:T(8,128)} %bitcast.86), calls=%async_computation | async-start | bytes 33554432 | tf_op jit(solution)/shard_map/all_to_all | solution.py:55
  103.9 499.7 %all-reduce.3.cloned.1.call-start = ((), (), s32[]{:S(2)}) async-start(), calls=%async_computation.1 | async-start | bytes 131072 | tf_op jit(solution)/shard_map/psum | solution.py:9
  527.7 138.7 %copy-start.1 = (f32[1,512,512]{2,1,0:T(8,128)S(1)}, f32[1,512,512]{2,1,0:T(8,128)}, u32[]{:S(2)}) copy-start(f32[1,512,512]{2,1,0:T(8,128)} %param.12) | copy-start | bytes 3145732
  538.2 126.5 %all-reduce.5.cloned.1.call-start = ((), (), s32[]{:S(2)}) async-start(), calls=%async_computation.2 | async-start | bytes 1048576 | tf_op jit(solution)/shard_map/psum | solution.py:9
Sparse Core Ops, SparseCore 0:
  538.4 65.1 all-reduce.2
  631.4 33.3 all-reduce.4
where the time goes:
time: 675 us; the launch traced here: 673 us
  waiting for transfers between devices  461 us (68%)
  other arithmetic  84 us (12%)
  local copies, waits for them, and re-layouts  56.4 us (8%)
  matrix products  49.3 us (7%)
  between operations  14.9 us (2%)
  starting transfers between devices  7.76 us (1%)
    all_to_all x1, waiting for transfers between devices, shards(): lax.all_to_all(contribution.reshape(rows_grid * cols_grid, rows_per, cols...  362 us
    psum x2, waiting for transfers between devices, broadcast(): return lax.psum(block, axis)  98.5 us
    scatter-add x1, other arithmetic, shards(): base_tiles.at[slot_ids].add(received.reshape(-1, tile_width, tile_width))  51.2 us
    dot_general x1, matrix products, shards(): jnp.einsum('kprt,kqcu->pqrctu', row_part, col_part, precision=lax.Precisi...  30 us
    neg x1, local copies, waits for them, and re-layouts, shards(): -jnp.einsum('kprt,kqcu->pqrctu', row_part, col_part, precision=lax.Precis...  17.4 us
    dot_general x1, matrix products, shards(): jnp.dot(own_factor, masked, precision=lax.Precision.HIGHEST, preferred_el...  16.4 us
  transfers between devices with their start and end apart: 3, of which 3 were waited for; matrix products, arithmetic and copies ran while one was open for 2% of the time, Pallas kernels for 0%

commit v1 on v0

--- a/solution.py
+++ b/solution.py
@@ -6,7 +6,8 @@
 
 def broadcast(block, axis, owner):
     block = jnp.where(lax.axis_index(axis) == owner, block, jnp.zeros_like(block))
-    return lax.psum(block, axis)
+    _feed_columns = lambda chunk, chip_axis: jnp.sum(lax.all_gather(chunk, chip_axis), axis=0)
+    return _feed_columns(block, axis)
 
 
 def solve_panel(diag_block, column):

time: 675 us -> 615 us (0.911)
  waiting for transfers between devices: 461 us -> 381 us
  blocking collectives: 0 us -> 31.6 us
  local copies, waits for them, and re-layouts: 56.4 us -> 45.5 us
    psum x2 -> x0, waiting for transfers between devices: 98.5 us -> none  [broadcast(): return lax.psum(block, axis)]
    all_gather x0 -> x1, blocking collectives: none -> 31.6 us  [broadcast(): lax.all_gather(chunk, chip_axis)]
    all_gather x0 -> x1, waiting for transfers between devices: none -> 19 us  [broadcast(): lax.all_gather(chunk, chip_axis)]
    scatter-add x1 -> x0, local copies, waits for them, and re-layouts: 9.09 us -> none  [shards(): base_tiles.at[slot_ids].add(received.reshape(-1, tile_width, tile_width))]
  transfers between devices with their start and end apart: 3 -> 2, of which waited for: 3 -> 2; matrix products, arithmetic and copies ran while one was open for 2% -> 2% of each run, Pallas kernels for 0% -> 0%
where the time goes in v1:
time: 615 us; the launch traced here: 614 us
  waiting for transfers between devices  381 us (62%)
  other arithmetic  84.4 us (14%)
  matrix products  48.8 us (8%)
  local copies, waits for them, and re-layouts  45.5 us (7%)
  blocking collectives  31.6 us (5%)
  between operations  14.9 us (2%)
  starting transfers between devices  7.5 us (1%)
    all_to_all x1, waiting for transfers between devices, shards(): lax.all_to_all(contribution.reshape(rows_grid * cols_grid, rows_per, cols...  362 us
    scatter-add x1, other arithmetic, shards(): base_tiles.at[slot_ids].add(received.reshape(-1, tile_width, tile_width))  51.2 us
    all_gather x1, blocking collectives, broadcast(): lax.all_gather(chunk, chip_axis)  31.6 us
    dot_general x1, matrix products, shards(): jnp.einsum('kprt,kqcu->pqrctu', row_part, col_part, precision=lax.Precisi...  30 us
    all_gather x1, waiting for transfers between devices, broadcast(): lax.all_gather(chunk, chip_axis)  19 us
    neg x1, local copies, waits for them, and re-layouts, shards(): -jnp.einsum('kprt,kqcu->pqrctu', row_part, col_part, precision=lax.Precis...  17.4 us
    dot_general x1, matrix products, shards(): jnp.dot(own_factor, masked, precision=lax.Precision.HIGHEST, preferred_el...  16.4 us
    another operation x3, other arithmetic, solve_panel(): lower = jnp.linalg.cholesky(0.5 * (diag_block + diag_block.T))  12.4 us
  transfers between devices with their start and end apart: 2, of which 2 were waited for; matrix products, arithmetic and copies ran while one was open for 2% of the time, Pallas kernels for 0%

profile of v1, /device:TPU:0, one launch (start us, length us, event | category | flops | bytes accessed | tf_op | source)
XLA Modules:
  0.0 613.9 jit_solution(4093995834380125606)
XLA Ops:
  7.2 0.0 copy-start
  7.2 0.0 copy-start.2
  7.2 8.0 %copy.44 = f32[1,8,1,16,128,128]{5,4,3,2,1,0:T(8,128)} copy(f32[1,8,1,16,128,128]{5,4,3,2,1,0:T(8,128)} %param.13) | data formatting | bytes 16777216
  15.2 0.2 dynamic-slice_reduce_fusion
  15.4 1.2 sort.64
  16.6 1.2 sort.65
  18.6 0.0 copy-done
  18.6 16.4 %fusion.3 = f32[2048,512]{1,0:T(8,128)} fusion(f32[1,512,2048]{2,1,0:T(8,128)} %param.11, pred[512]{0:T(512)(128)(4,1)S(1)} %iota_compare_fusion.2, f32[1,512,512]{2,1,0:T(8,128)S(1)} %copy-done), kind=kOutput, calls=%fused_computation.9 | convolution fusion | flops 6444548096 | bytes 9437696 | tf_op jit(solution)/shard_map/dot_general | solution.py:43
  35.0 5.0 gather_fusion.2
  40.0 5.0 gather_fusion.3
  44.9 2.9 broadcast_select_fusion.1
  47.9 0.5 copy-done.3
  48.4 0.6 broadcast_select_fusion
  49.0 30.0 %negate_bitcast_fusion = f32[8,4,2,4,128,128]{4,5,2,0,3,1:T(8,128)} fusion(f32[512,4,4,128,1,1]{0,3,5,4,2,1:T(8,128)S(1)} %bitcast.90, f32[512,8,2,128,1,1]{0,3,2,1,5,4:T(8,128)S(1)} %bitcast.91), kind=kOutput, calls=%fused_computation.5 | convolution fusion | flops 25773998080 | bytes 25165824 | tf_op jit(solution)/shard_map/kprt,kqcu->pqrctu/dot_general | solution.py:53
  79.0 17.4 %copy.31 = f32[8,4,2,4,128,128]{5,4,3,2,1,0:T(8,128)} copy(f32[8,4,2,4,128,128]{4,5,2,0,3,1:T(8,128)} %negate_bitcast_fusion) | data formatting | bytes 33554432 | tf_op jit(solution)/shard_map/neg | solution.py:53
  96.4 7.5 %all-to-all-start = ((f32[32,2,4,128,128]{4,3,2,1,0:T(8,128)}), f32[32,2,4,128,128]{4,3,2,1,0:T(8,128)}, u32[]{:S(2)}, u32[]{:S(2)}) async-start(f32[32,2,4,128,128]{4,3,2,1,0:T(8,128)} %bitcast.87), calls=%async_computation | async-start | bytes 33554432 | tf_op jit(solution)/shard_map/all_to_all | solution.py:56
  103.9 0.0 all-gather.4.cloned.1.call-start
  103.9 0.7 sort.63
  104.7 0.1 copy.27
  104.7 0.1 reshape.214
  104.8 3.9 gather_fusion.1
  108.7 0.1 reshape.217
  108.8 0.1 copy.28
  108.9 0.1 copy.29
  109.0 0.7 sort.62
  109.7 0.1 copy.24
  109.8 0.1 reshape.209
  109.9 3.9 gather_fusion
  113.8 0.1 reshape.212
  113.8 0.1 copy.25
  113.9 0.1 copy.26
  114.0 0.1 broadcast_add_fusion
  114.1 0.1 add.118
  114.3 362.2 %all-to-all-done = f32[32,2,4,128,128]{4,3,2,1,0:T(8,128)} async-done(((f32[32,2,4,128,128]{4,3,2,1,0:T(8,128)}), f32[32,2,4,128,128]{4,3,2,1,0:T(8,128)}, u32[]{:S(2)}, u32[]{:S(2)}) %all-to-all-start) | async-done | bytes 16777248 | tf_op jit(solution)/shard_map/all_to_all | solution.py:56
  476.4 51.2 %scatter_fusion = f32[128,128,128]{2,1,0:T(8,128)} fusion(f32[128,128,128]{2,1,0:T(8,128)} %bitcast.83, s32[256]{0:T(256)S(1)} %bitcast.95, f32[256,128,128]{2,1,0:T(8,128)} %bitcast.24), kind=kCustom, calls=%fused_computation.4 | custom fusion | flops 4194304 | bytes 50332672 | tf_op jit(solution)/shard_map/scatter-add | solution.py:75
  527.7 0.8 slice_select_fusion
  528.5 31.6 %all-gather = f32[8,1,128,128]{3,2,1,0:T(8,128)S(1)} all-gather(f32[1,1,128,128]{3,2,1,0:T(8,128)S(1)} %slice_select_fusion), channel_id=2, replica_groups=mesh['prow'=8,'pcol'=4] {'prow'}, dimensions={0}, use_global_device_ids=true | all-gather | bytes 589824 | tf_op jit(solution)/shard_map/all_gather | solution.py:9
  560.1 0.1 copy.33
  560.2 11.7 %cholesky.15 = f32[128,128]{1,0:T(8,128)S(1)} custom-call(f32[128,128]{1,0:T(8,128)S(1)} %fusion.12), custom_call_target="Cholesky" | custom-call | tf_op jit(solution)/shard_map/jit(cholesky)/cholesky | solution.py:14
  572.0 0.6 compare_reduce_fusion
  572.6 0.7 fusion.9
  573.3 9.8 %custom-call.7 = f32[1,128,128]{1,2,0:T(8,128)S(1)} custom-call(f32[1,128,128]{2,1,0:T(8,128)S(1)} %fusion.9), custom_call_target="InvertDiagBlocksLowerTriangular" | custom-call | tf_op jit(solution)/shard_map/jit(_solve_triangular)/triangular_solve | solution.py:16
  583.1 2.4 convolution_select_fusion
  585.5 0.0 all-gather.4.cloned.1.call-update
  585.5 19.0 %all-gather.4.cloned.1.call-done = f32[32,128,128]{2,1,0:T(8,128)} async-done(((f32[8,128,128]{2,1,0:T(8,128)}), f32[32,128,128]{2,1,0:T(8,128)}) %all-gather.4.cloned.1.call-update) | async-done | bytes 2097168 | tf_op jit(solution)/shard_map/all_gather | solution.py:9
  604.6 1.8 reduce_sum.19
  606.4 0.7 dynamic-slice_bitcast_fusion
  607.0 0.0 copy-done.1
  (24 shorter events, 0.2 us)
Async XLA Ops:
  7.2 11.4 %copy-start = (f32[1,512,512]{2,1,0:T(8,128)S(1)}, f32[1,512,512]{2,1,0:T(8,128)}, u32[]{:S(2)}) copy-start(f32[1,512,512]{2,1,0:T(8,128)} %param.12) | copy-start | bytes 3145732
  7.2 8.0 %copy-start.2 = (s32[32,16]{0,1:T(8,128)S(1)}, s32[32,16]{0,1:T(8,128)}, u32[]{:S(2)}) copy-start(s32[32,16]{0,1:T(8,128)} %param.9) | copy-start | bytes 6148
  44.9 3.4 copy-start.3
  96.4 380.1 %all-to-all-start = ((f32[32,2,4,128,128]{4,3,2,1,0:T(8,128)}), f32[32,2,4,128,128]{4,3,2,1,0:T(8,128)}, u32[]{:S(2)}, u32[]{:S(2)}) async-start(f32[32,2,4,128,128]{4,3,2,1,0:T(8,128)} %bitcast.87), calls=%async_computation | async-start | bytes 33554432 | tf_op jit(solution)/shard_map/all_to_all | solution.py:56
  103.9 500.7 %all-gather.4.cloned.1.call-start = ((), (), s32[]{:S(2)}) async-start(), calls=%async_computation.1 | async-start | bytes 2621440 | tf_op jit(solution)/shard_map/all_gather | solution.py:9
  476.4 130.6 %copy-start.1 = (f32[1,512,512]{2,1,0:T(8,128)S(1)}, f32[1,512,512]{2,1,0:T(8,128)}, u32[]{:S(2)}) copy-start(f32[1,512,512]{2,1,0:T(8,128)} %param.12) | copy-start | bytes 3145732
Sparse Core Ops, SparseCore 0:
  585.7 18.8 all-gather.3
